TPU v7x, 256 devices: a whole 4x4x8 slice. The times are simulated.
256 devices in a mesh: ctx: 16 (over z_hi, x), tp: 4 (over y), dp: 4 (over z_lo, core).
Axes of the slice: x: 4, y: 4, z: 8 (z_hi: 4, z_lo: 2; z = z_hi * 2 + z_lo), core: 2. Of those that a mesh axis runs over, the one named last changes fastest.
Arguments:
- byte_embed: bfloat16 [65536, 1024], P(('dp', 'ctx', 'tp')), parts along dimension 0, may hold values from -6 to 6
- patch_start: int32 [65536], P(('dp', 'ctx', 'tp')), parts along dimension 0, may hold values from 0 to 1, as said below
- enc_gain: float32 [1024], replicated, may hold values from 0.1 to 1.9
- enc_qkv: bfloat16 [1024, 3072], replicated, may hold values from -4 to 4
- enc_out: bfloat16 [1024, 1024], replicated, may hold values from -0.1875 to 0.1875
- up_proj: bfloat16 [1024, 4096], P('ctx', 'tp'), may hold values from -0.1875 to 0.1875
- lat_gain: float32 [4096], replicated, may hold values from 0.1 to 1.9
- query_proj: bfloat16 [4096, 2048], P('ctx', 'tp'), may hold values from -4 to 4
- key_proj: bfloat16 [4096, 512], P('ctx', 'tp'), may hold values from -4 to 4
- value_matrix: bfloat16 [4096, 512], P('ctx', 'tp'), may hold values from -0.09375 to 0.09375
- out_proj: bfloat16 [2048, 4096], P('tp', 'ctx'), may hold values from -0.125 to 0.125
- down_proj: bfloat16 [4096, 1024], P('tp', 'ctx'), may hold values from -0.09375 to 0.09375
Outputs:
- byte_states: bfloat16 [65536, 1024], P(('dp', 'ctx', 'tp')), parts along dimension 0
There are 4 independent parts, one for each index of `dp`. A program takes and returns all parts, laid end to end along the dimension named above; an argument that names none is the same for every part. Nothing has to cross between parts.
Inputs may be any that keep to these rules, and one draw needn't show every extreme that they name: `patch_start`: byte 0 begins a patch; every patch spans 1 to 19 bytes; each aligned group of 1024 bytes holds at most 256 patch starts, and some group holds exactly 256.
All inputs are finite; a program needn't handle non-finite values.
Results may differ from a plain program's by a relative error of at most 0.015.
Values may be sent and summed in bfloat16 or wider, within the bound.
A program may use at most 128 MiB of HBM per device.

v0:
```python
import heapq

import jax
import jax.numpy as jnp
from jax import lax
from jax.experimental import pallas as pl
from jax.experimental.pallas import tpu as pltpu
from jax.sharding import PartitionSpec as P

BH = 16
HB = 64
HEAD_SIZE = 128
WIN = 512
EPS = 1e-05
MESH = pl.DeviceIdType.MESH
BF = jnp.bfloat16
F32 = jnp.float32
ROWS = 1792
HALF = ROWS // 2
A_ROWS = 448


def gather_plan(rate=46.6e3, latency=2.0):
    sizes = {"A": A_ROWS, "B": HALF - A_ROWS}
    free = {link: 0.0 for link in ("E", "I", "X+", "X-", "D")}
    heap, order, sends, halves = [], [], [], {}

    def send(now, kind, dz, dx, half, link, batch):
        rows = sizes[kind] // (1 if half is None else 2)
        end = max(now, free[link]) + rows * 512 / (650e3 if link == "D" else rate)
        free[link] = end
        sends.append((kind, dz, dx, half, link))
        batch.append(len(sends) - 1)
        heapq.heappush(heap, (end + (1.0 if link == "D" else latency), len(sends) - 1))

    def have(now, kind, dz, dx, batch):
        if kind == "A" and dx == 0:
            if dz == 0:
                send(now, "A", 0, 0, None, "E", batch)
            elif dz == 1:
                send(now, "A", 1, 0, None, "I", batch)
            elif dz == -1:
                send(now, "A", -1, 0, "other", "E", batch)
            send(now, "A", dz, 0, None, "X+", batch)
            send(now, "A", dz, 0, None, "X-", batch)
        elif kind == "A" and dx == -1:
            send(now, "A", dz, -1, 0, "X+", batch)
        elif kind == "A" and dx == 1:
            send(now, "A", dz, 1, 1, "X-", batch)
        elif kind == "B" and dz == 0:
            if dx == 0:
                send(now, "B", 0, 0, None, "X+", batch)
                send(now, "B", 0, 0, None, "X-", batch)
            elif dx == -1:
                send(now, "B", 0, -1, 0, "X+", batch)
            elif dx == 1:
                send(now, "B", 0, 1, 1, "X-", batch)
            send(now, "B", 0, dx, None, "E", batch)
        elif kind == "B" and dz == 1:
            send(now, "B", 1, dx, None, "I", batch)
        elif kind == "B" and dz == -1:
            send(now, "B", -1, dx, "other", "E", batch)
        if (dz, dx) != (0, 0):
            send(now, kind, dz, dx, None, "D", batch)

    first = []
    have(0.0, "A", 0, 0, first)
    have(0.0, "B", 0, 0, first)
    order.append((None, first))
    while heap:
        now, k = heapq.heappop(heap)
        kind, dz, dx, half, link = sends[k]
        batch = []
        if link != "D":
            if link == "E":
                dz = 1 if dz == 0 else 2
            elif link == "I":
                dz = {1: -1, 2: 2}[dz]
            elif link == "X+":
                dx = {0: -1, -1: 2}[dx]
            else:
                dx = {0: 1, 1: 2}[dx]
            if half is None:
                have(now, kind, dz, dx, batch)
            else:
                key = (kind, dz, dx)
                halves[key] = halves.get(key, 0) + 1
                if link == "E":
                    send(now, kind, 2, dx, "mine", "I", batch)
                if halves[key] == 2:
                    have(now, kind, dz, dx, batch)
        order.append((k, batch))
    return order, sends


ORDER, SENDS = gather_plan()


def enter(devices):
    barrier = pltpu.get_barrier_semaphore()
    for device in devices:
        pl.semaphore_signal(barrier, inc=1, device_id=device, device_id_type=MESH)
    pl.semaphore_wait(barrier, len(devices))


def position():
    return lax.axis_index("ctx"), lax.axis_index("tp"), lax.axis_index("dp")


def remote(src, dst, send, recv, device):
    return pltpu.make_async_remote_copy(
        src_ref=src, dst_ref=dst, send_sem=send, recv_sem=recv, device_id=device, device_id_type=MESH
    )


def normal(rows, gain):
    floats = rows.astype(F32)
    return (floats * lax.rsqrt(jnp.mean(floats * floats, axis=-1, keepdims=True) + EPS) * gain).astype(BF)


def nt(a, b):
    return lax.dot_general(a, b, (((1,), (1,)), ((), ())), preferred_element_type=F32)


def first_kernel(
    up, query_w, key_w, value_w, out_w, down_t, embed, count, gain, qkv_hbm, out_hbm,
    whole, hidden, counts,
    own, halo, relay, qkv, enc_out, normed, query, keyval, mixed, bias,
    own_sem, w_sem, g_send, g_recv, h_send, h_recv, r_send, r_recv, x_send, x_recv, c_send, c_recv,
):
    ctx, tp, dp = position()
    h, x, lo, core = ctx // 4, ctx % 4, dp // 2, dp % 2
    way = 2 * lo - 1
    turned = (1 - lo) * 2 + core
    link = {
        "E": (((h + way + 4) % 4) * 4 + x, tp, turned),
        "I": (ctx, tp, turned),
        "X+": (h * 4 + (x + 1) % 4, tp, dp),
        "X-": (h * 4 + (x + 3) % 4, tp, dp),
        "D": (ctx, tp, lo * 2 + 1 - core),
    }
    loads = [pltpu.make_async_copy(up.at[:, pl.ds(256 * i, 256)], own.at[pl.ds(64 * i, 64)], own_sem.at[i]) for i in range(4)]
    loads += [
        pltpu.make_async_copy(query_w.at[:, pl.ds(256 * i, 256)], own.at[pl.ds(256 + 256 * i, 256)], own_sem.at[4 + i])
        for i in range(2)
    ]
    loads.append(pltpu.make_async_copy(key_w, own.at[pl.ds(768, 256), pl.ds(0, 128)], own_sem.at[6]))
    loads.append(pltpu.make_async_copy(value_w, own.at[pl.ds(768, 256), pl.ds(128, 128)], own_sem.at[7]))
    loads.append(pltpu.make_async_copy(out_w, own.at[pl.ds(1024, 512)], own_sem.at[8]))
    loads += [
        pltpu.make_async_copy(down_t.at[:, pl.ds(256 * i, 256)], own.at[pl.ds(1536 + 64 * i, 64)], own_sem.at[9 + i])
        for i in range(4)
    ]
    for load in loads:
        load.start()
    weights = [pltpu.make_async_copy(qkv_hbm, qkv, w_sem.at[0]), pltpu.make_async_copy(out_hbm, enc_out, w_sem.at[1])]
    for load in weights:
        load.start()

    def copy(k):
        kind, dz, dx, half, where = SENDS[k]
        rows = A_ROWS if kind == "A" else HALF - A_ROWS
        base = core * HALF + (0 if kind == "A" else A_ROWS)
        if half is not None:
            rows = rows // 2
            base = base + {"mine": lo, "other": 1 - lo}.get(half, half) * rows
        part = pl.ds(pl.multiple_of(base, 16), rows)
        piece = whole.at[(h + dz * way + 8) % 4, (x + dx + 4) % 4, part]
        return remote(own.at[part] if (dz, dx) == (0, 0) else piece, piece, g_send.at[k], g_recv.at[k], link[where])

    last = (tp == 3).astype(jnp.int32)
    zero = (tp == 0).astype(jnp.int32)
    following = ((ctx + last) % 16, (tp + 1) % 4, dp)
    previous = ((ctx - zero + 16) % 16, (tp + 3) % 4, dp)
    tps = [(ctx, (tp + i) % 4, dp) for i in (1, 2, 3)]
    over = ((((h + 1) % 4) * 4), tp * 0, dp)
    under = [((((h + 3) % 4) * 4 + j), t, dp) for t in (2, 3) for j in range(4)]
    row_mates = [(h * 4 + j, tp, dp) for j in range(3)]
    origin = (h * 4 + 3, tp, dp)
    upper = tp >= 2
    sends_over = (x == 3) & upper
    relays = (x < 3) & upper
    takes_over = (x == 0) & (tp == 0)
    crossing = (x == 3) & (tp == 3)

    barrier = pltpu.get_barrier_semaphore()

    def greet(devices):
        for device in devices:
            pl.semaphore_signal(barrier, inc=1, device_id=device, device_id_type=MESH)

    greet([link[name] for name in ("E", "I", "X+", "X-", "D")] + [following, previous] + tps)

    @pl.when(sends_over)
    def _():
        greet(row_mates + [over])

    @pl.when(relays)
    def _():
        greet([origin, over])

    @pl.when(takes_over)
    def _():
        greet(under)

    more = 4 * sends_over.astype(jnp.int32) + 2 * relays.astype(jnp.int32) + 8 * takes_over.astype(jnp.int32)
    pl.semaphore_wait(barrier, 10 + more)

    one = remote(embed, halo.at[1], h_send.at[0], h_recv.at[0], following)
    two = remote(halo.at[1], halo.at[0], h_send.at[1], h_recv.at[1], following)
    to_relay = [remote(embed.at[pl.ds(64 * j, 64)], relay, r_send.at[j], r_recv, row_mates[j]) for j in range(3)]

    def over_copy(t, j):
        src = embed.at[pl.ds(192, 64)] if j == 3 else relay
        return remote(src, halo.at[t - 2, pl.ds(64 * j, 64)], x_send, x_recv.at[4 * (t - 2) + j], over)

    def each_over(action, columns):
        for t in (2, 3):
            for j in columns:

                @pl.when((tp == t) & (x == j))
                def _():
                    action(over_copy(t, j))

    @pl.when(sends_over)
    def _():
        for c in to_relay:
            c.start()

    each_over(lambda c: c.start(), (3,))

    @pl.when(jnp.logical_not(crossing))
    def _():
        one.start()

    for i, device in enumerate(tps):
        remote(count, counts.at[tp], c_send.at[i], c_recv.at[i], device).start()
    counts[pl.ds(tp, 1)] = count[...][None]

    def first_sends():
        for load in loads:
            load.wait()
        for s in ORDER[0][1]:
            copy(s).start()

    def project(block, rows, columns):
        normed[...] = normal(rows, gain[...])

        def tile(i, carry):
            at = pl.multiple_of(i * 256, 256)
            piece = jnp.dot(normed[...], qkv[:, pl.ds(1024 + at, 256)], preferred_element_type=F32).astype(BF)
            keyval[pl.ds(256 * block, 256), pl.ds(at, 256)] = piece
            return carry

        lax.fori_loop(0, 8, tile, 0)
        if columns:

            def query_tile(i, carry):
                at = pl.multiple_of(i * 256, 256)
                piece = jnp.dot(normed[...], qkv[:, pl.ds(at, 256)], preferred_element_type=F32)
                query[:, pl.ds(at, 256)] = (piece.astype(BF).astype(F32) * 0.125).astype(BF)
                return carry

            lax.fori_loop(0, 4, query_tile, 0)

    def own_part():
        r = lax.broadcasted_iota(jnp.int32, (256, 768), 0)
        c = lax.broadcasted_iota(jnp.int32, (256, 768), 1)
        floor = 512 - 256 * (ctx * 4 + tp)
        bias[...] = jnp.where((c <= r + 512) & (c > r) & (c >= floor), F32(0.0), F32(-1e30))
        weights[0].wait()
        project(2, embed[...], True)

    def relay_part():
        @pl.when(relays)
        def _():
            remote(embed.at[pl.ds(0, 64)], relay, r_send.at[0], r_recv, origin).wait_recv()

        each_over(lambda c: c.start(), (0, 1, 2))

    def near_part():
        @pl.when(jnp.logical_not(takes_over))
        def _():
            one.wait_recv()

        @pl.when(takes_over)
        def _():
            for j in range(4):
                over_copy(3, j).wait_recv()

        @pl.when(jnp.logical_not(crossing))
        def _():
            two.start()

        project(1, halo[1], False)

    def far_part():
        @pl.when(jnp.logical_not(takes_over))
        def _():
            two.wait_recv()

        @pl.when(takes_over)
        def _():
            for j in range(4):
                over_copy(2, j).wait_recv()

        project(0, halo[0], False)

    lanes = lax.broadcasted_iota(jnp.int32, (256, 128), 1)

    def attend(pair):
        at = pl.ds(128 * pair, 128)
        both = query[:, at]
        k = keyval[:, at]
        v = keyval[:, pl.ds(1024 + 128 * pair, 128)]
        outs = []
        for side in range(2):
            q = jnp.where((lanes < 64) == (side == 0), both, jnp.zeros_like(both))
            s = nt(q, k) + bias[...]
            e = jnp.exp(s - jnp.max(s, axis=-1, keepdims=True))
            total = jnp.sum(e, axis=-1, keepdims=True)
            outs.append(jnp.dot(e.astype(BF), v, preferred_element_type=F32) / total)
        mixed[:, at] = jnp.where(lanes < 64, outs[0], outs[1]).astype(BF)

    def finish():
        weights[1].wait()

        def tile(i, carry):
            at = pl.ds(pl.multiple_of(i * 256, 256), 256)
            piece = jnp.dot(mixed[...], enc_out[:, at], preferred_element_type=F32)
            hidden[:, at] = (embed[:, at].astype(F32) + piece).astype(BF)
            return carry

        lax.fori_loop(0, 4, tile, 0)

    jobs = {0: [own_part], 3: [relay_part], 14: [near_part], FAR: [far_part]}
    for pair in range(8):
        jobs.setdefault(FAR + 2 + 2 * pair, []).append(lambda pair=pair: attend(pair))
    jobs.setdefault(FAR + 18, []).append(finish)
    first_sends()
    keep = pltpu.make_async_copy(own, whole.at[h, x], w_sem.at[2])
    keep.start()
    done = []
    for step, (k, batch) in enumerate(ORDER):
        if step > 0:
            copy(k).wait_recv()
            for s in batch:
                copy(s).start()
        for job in jobs.get(step, []):
            job()
            done.append(job)
    for step in sorted(jobs):
        for job in jobs[step]:
            if job not in done:
                job()
    keep.wait()

    @pl.when(jnp.logical_not(crossing))
    def _():
        one.wait_send()
        two.wait_send()

    @pl.when(sends_over)
    def _():
        for c in to_relay:
            c.wait_send()

    each_over(lambda c: c.wait_send(), (0, 1, 2, 3))
    for i, device in enumerate(tps):
        remote(count, counts.at[tp], c_send.at[i], c_recv.at[i], device).wait()
    for k in range(len(SENDS)):
        copy(k).wait_send()


FAR = 46


def first_stage(up, query_w, key_w, value_w, out_w, down_t, embed, count, gain, qkv, enc_out):
    anywhere = pl.BlockSpec(memory_space=pl.ANY)
    vmem = pl.BlockSpec(memory_space=pltpu.VMEM)
    n = len(SENDS)
    dma = pltpu.SemaphoreType.DMA
    return pl.pallas_call(
        first_kernel,
        out_shape=(
            jax.ShapeDtypeStruct((4, 4, ROWS, 256), BF),
            jax.ShapeDtypeStruct(embed.shape, BF),
            jax.ShapeDtypeStruct((4, 8, 128), jnp.int32),
        ),
        in_specs=[anywhere] * 6 + [vmem] * 3 + [anywhere] * 2,
        out_specs=(anywhere, vmem, vmem),
        scratch_shapes=[
            pltpu.VMEM((ROWS, 256), BF),
            pltpu.VMEM((2, 256, 1024), BF),
            pltpu.VMEM((64, 1024), BF),
            pltpu.VMEM((1024, 3072), BF),
            pltpu.VMEM((1024, 1024), BF),
            pltpu.VMEM((256, 1024), BF),
            pltpu.VMEM((256, 1024), BF),
            pltpu.VMEM((768, 2048), BF),
            pltpu.VMEM((256, 1024), BF),
            pltpu.VMEM((256, 768), F32),
            dma((13,)), dma((3,)), dma((n,)), dma((n,)), dma((2,)), dma((2,)), dma((3,)), dma, dma, dma((8,)),
            dma((3,)), dma((3,)),
        ],
        compiler_params=pltpu.CompilerParams(collective_id=0, has_side_effects=True, vmem_limit_bytes=62 * 2**20),
    )(up, query_w, key_w, value_w, out_w, down_t, embed, count, gain, qkv, enc_out)


def second_kernel(
    hidden, marks_row, marks_col, counts, gain, weights_hbm,
    out,
    w, ones, parts, arrived, share, pooled, latent, scaled, acc, kv, kv_all, query, mx, tot, mix, attn,
    far, relay_r, relay_l, to_right, to_left, arr_r, arr_l, lat_out, downs, down_in, down_share, patch,
    lead, lead_in, trail, trail_in,
    w_sem, p_send, p_recv, s_send, s_recv, l_send, l_recv, f_send, f_recv, z_send, z_recv, x_send, x_recv,
    o_send, o_recv, d_send, d_recv, e_send, e_recv, lead_send, lead_recv, trail_send, trail_recv,
):
    ctx, tp, dp = position()
    h, x = ctx // 4, ctx % 4
    load = pltpu.make_async_copy(weights_hbm, w, w_sem)
    load.start()
    tps = [(ctx, (tp + i) % 4, dp) for i in (1, 2, 3)]
    up_y, down_y = tps[0], tps[2]
    zs = [(((h + i) % 4) * 4 + x, tp, dp) for i in (1, 3, 2)]
    right, left = (h * 4 + (x + 1) % 4, tp, dp), (h * 4 + (x + 3) % 4, tp, dp)
    next_first = ((ctx + 1) % 16, tp * 0, dp)
    before_all = [((ctx + 15) % 16, t, dp) for t in range(4)]
    barrier = pltpu.get_barrier_semaphore()

    def greet(devices):
        for device in devices:
            pl.semaphore_signal(barrier, inc=1, device_id=device, device_id_type=MESH)

    greet(tps + zs + [right, left, next_first])

    @pl.when(tp == 0)
    def _():
        greet(before_all)

    def dot(a, b):
        return jnp.dot(a, b, preferred_element_type=F32)

    def iota(shape, dim):
        return lax.broadcasted_iota(jnp.int32, shape, dim).astype(F32)

    ones[...] = jnp.ones_like(ones)
    r256, c256 = iota((256, 256), 0), iota((256, 256), 1)
    c4 = [counts[t].astype(F32) for t in range(4)]
    offset = jnp.zeros((8, 128), F32)
    for t in range(4):
        offset = offset + jnp.where(tp > t, c4[t], F32(0.0))
    group = c4[0] + c4[1] + c4[2] + c4[3]
    offset, group_one = offset[0:1, 0:1], group[0:1, 0:1]
    run_row = dot(marks_row[...], (r256 <= c256).astype(BF))
    run_col = dot((r256 >= c256).astype(BF), marks_col[...])[:, 0:1]
    slot_row = run_row[0:1] + offset - 1.0
    slot_col = run_col + offset - 1.0
    place = (r256 == slot_row).astype(BF)
    mass = dot(place, hidden[...])
    number = dot(place, ones[...])
    for t in range(4):
        parts[t, :, pl.ds(0, 1024)] = mass[64 * t : 64 * t + 64].astype(BF)
        parts[t, :, pl.ds(1024, 128)] = number[64 * t : 64 * t + 64].astype(BF)
    leading = (run_row == 0.0).astype(BF)
    lead[:, pl.ds(0, 1024)] = dot(leading, hidden[...])
    lead[:, pl.ds(1024, 128)] = dot(leading, ones[...])

    pl.semaphore_wait(barrier, 9 + 4 * (tp == 0).astype(jnp.int32))

    leads = [remote(lead, lead_in, lead_send.at[t], lead_recv, before_all[t]) for t in range(4)]

    @pl.when(tp == 0)
    def _():
        for c in leads:
            c.start()

    def scatter(src, dst, send, recv):
        return [remote(src.at[(tp + i + 1) % 4], dst.at[tp], send.at[i], recv.at[i], tps[i]) for i in range(3)]

    def spread(src, dst, send, recv):
        return [remote(src, dst.at[tp], send.at[i], recv.at[i], tps[i]) for i in range(3)]

    first = scatter(parts, arrived, p_send, p_recv)
    for c in first:
        c.start()
    arrived[pl.ds(tp, 1)] = parts[pl.ds(tp, 1)]
    for c in first:
        c.wait_recv()
    leads[0].wait_recv()
    sums = arrived[0].astype(F32) + arrived[1].astype(F32) + arrived[2].astype(F32) + arrived[3].astype(F32)
    my_row = iota((64, 1152), 0) + (64 * tp).astype(F32)
    sums = sums + jnp.where(my_row == group_one - 1.0, lead_in[0:1], F32(0.0))
    share[...] = (sums[:, :1024] / jnp.maximum(sums[:, 1024:1025], 1.0)).astype(BF)
    second = spread(share, pooled, s_send, s_recv)
    for c in second:
        c.start()
    pooled[pl.ds(tp, 1)] = share[...][None]
    load.wait()
    for c in second:
        c.wait_recv()

    def columns(t, i):
        return pl.ds(pl.multiple_of(1024 * t + 256 * i, 256), 256)

    def sent(i):
        block = latent.at[:, columns(tp, i)]
        return [
            remote(block, block, l_send.at[i], l_recv.at[i], up_y),
            remote(block, block, l_send.at[4 + i], l_recv.at[4 + i], down_y),
        ]

    def passed(i):
        block = latent.at[:, columns((tp + 3) % 4 if i < 2 else (tp + 1) % 4, i)]
        return remote(block, block, f_send.at[i], f_recv.at[i], up_y if i < 2 else down_y)

    all_pooled = pooled[...].reshape(256, 1024)
    for i in range(4):
        block = w[:, :, pl.ds(64 * i, 64), :].reshape(1024, 256)
        latent[:, columns(tp, i)] = dot(all_pooled, block).astype(BF)
        for c in sent(i):
            c.start()

    def contract(t, i, fresh=False):
        values = latent[:, columns(t, i)].astype(F32)
        inputs = (values * gain[:, columns(t, i)]).astype(BF)
        power = jnp.sum(values * values, axis=-1, keepdims=True)
        scaled[...] = power if fresh else scaled[...] + power
        for b in range(3):
            term = dot(inputs, w[t, i, pl.ds(256 + 256 * b, 256), :])
            acc[b] = term if fresh else acc[b] + term

    for i in range(4):
        contract(tp, i, i == 0)
    for i in range(4):
        remote(latent.at[:, columns(tp, i)], latent.at[:, columns(tp, i)], l_send.at[i], l_recv.at[i], up_y).wait_recv()
        if i < 2:
            passed(i).start()
        remote(latent.at[:, columns(tp, i)], latent.at[:, columns(tp, i)], l_send.at[4 + i], l_recv.at[4 + i], down_y).wait_recv()
        if i >= 2:
            passed(i).start()
        contract((tp + 3) % 4, i)
        contract((tp + 1) % 4, i)
    for i in (0, 2, 1, 3):
        passed(i).wait_recv()
        contract((tp + 2) % 4, i)
    scale = lax.rsqrt(scaled[...] * F32(1.0 / 4096.0) + EPS)
    kv[pl.ds(0, 256)] = (acc[2] * scale).astype(BF)
    kv[pl.ds(256, 16)] = jnp.broadcast_to(group_one, (16, 256)).astype(BF)

    z_copies = [remote(kv, kv_all.at[h, x], z_send.at[i], z_recv.at[i], zs[i]) for i in range(3)]
    for c in z_copies:
        c.start()

    def across(j, dz):
        z = (h + dz) % 4
        src = kv if dz == 0 else kv_all.at[z, x]
        lower, upper = pl.ds(0, 128), pl.ds(128, 144)
        a, b = (x + 3) % 4, (x + 1) % 4
        return [
            remote(src, kv_all.at[z, x], x_send.at[4 * j], x_recv.at[4 * j], right),
            remote(src, kv_all.at[z, x], x_send.at[4 * j + 1], x_recv.at[4 * j + 1], left),
            remote(kv_all.at[z, a, lower], kv_all.at[z, a, lower], x_send.at[4 * j + 2], x_recv.at[4 * j + 2], right),
            remote(kv_all.at[z, b, upper], kv_all.at[z, b, upper], x_send.at[4 * j + 3], x_recv.at[4 * j + 3], left),
        ]

    turns = (0, 3, 1, 2)
    sets = [across(j, dz) for j, dz in enumerate(turns)]
    sets[0][0].start()
    sets[0][1].start()
    kv_all[pl.ds(h, 1), pl.ds(x, 1)] = kv[...][None, None]
    for head in range(4):
        q = acc[head // 2][:, 128 * (head % 2) : 128 * (head % 2) + 128] * scale
        query[head] = q.astype(BF)

    shrink = F32(1.0) / jnp.sqrt(F32(HEAD_SIZE))

    def attend(dz, dx, fresh=False):
        z, xx = (h + dz) % 4, (x + dx) % 4
        other = z * 4 + xx

        @pl.when(other <= ctx)
        def _():
            keys = kv_all[z, xx, pl.ds(0, 256), pl.ds(0, 128)]
            values = kv_all[z, xx, pl.ds(0, 256), pl.ds(128, 128)]
            limit = kv_all[z, xx, pl.ds(256, 16), :][0:1].astype(F32)
            allowed = c256 < limit
            if fresh:
                allowed = allowed & (c256 <= r256)
            bias = jnp.where(allowed, F32(0.0), F32(-1e30))

            def one_head(head, carry):
                s = nt(query[head], keys) * shrink + bias
                peak = jnp.max(s, axis=-1, keepdims=True)
                if not fresh:
                    old = mx[head]
                    peak = jnp.maximum(peak, old)
                e = jnp.exp(s - peak)
                total = jnp.sum(e, axis=-1, keepdims=True)
                mixed = dot(e.astype(BF), values)
                if not fresh:
                    fade = jnp.exp(old - peak)
                    total = total + tot[head] * fade
                    mixed = mixed + mix[head] * fade
                mx[head] = peak
                tot[head] = total
                mix[head] = mixed
                return carry

            lax.fori_loop(0, 4, one_head, 0)

    attend(0, 0, True)
    for j in range(4):
        if j > 0:
            z_copies[j - 1].wait_recv()
            sets[j][0].start()
            sets[j][1].start()
            for i in (0, 1):
                sets[j - 1][i].wait_recv()
                sets[j - 1][i + 2].start()
            attend(turns[j], 0)
            attend(turns[j - 1], 3)
            attend(turns[j - 1], 1)
    for i in (0, 1):
        sets[3][i].wait_recv()
        sets[3][i + 2].start()
    attend(turns[3], 3)
    attend(turns[3], 1)
    for j in range(4):
        for i in (2, 3):
            sets[j][i].wait_recv()
        attend(turns[j], 2)
    for head in range(4):
        attn[:, pl.ds(128 * head, 128)] = (mix[head] / tot[head]).astype(BF)

    def part(t, i):
        return dot(attn[...], w[t, i, pl.ds(1024, 512), :])

    def block(i):
        return pl.ds(256 * i, 256)

    opposite, above, below = (tp + 2) % 4, (tp + 1) % 4, (tp + 3) % 4
    low, high = pl.ds(0, 128), pl.ds(128, 128)
    for i in range(4):
        far[:, block(i)] = part(opposite, i).astype(BF)
    o_copies = [
        remote(far.at[low], relay_r, o_send.at[0], o_recv.at[0], up_y),
        remote(far.at[high], relay_l, o_send.at[1], o_recv.at[1], down_y),
        remote(to_right, arr_r, o_send.at[2], o_recv.at[2], up_y),
        remote(to_left, arr_l, o_send.at[3], o_recv.at[3], down_y),
    ]
    o_copies[0].start()
    o_copies[1].start()
    for i in range(4):
        acc_r = part(above, i)
        if i == 0:
            o_copies[0].wait_recv()
        to_right[low, block(i)] = (acc_r[:128] + relay_r[:, block(i)].astype(F32)).astype(BF)
        to_right[high, block(i)] = acc_r[128:].astype(BF)
    o_copies[2].start()
    for i in range(4):
        acc_l = part(below, i)
        if i == 0:
            o_copies[1].wait_recv()
        to_left[low, block(i)] = acc_l[:128].astype(BF)
        to_left[high, block(i)] = (acc_l[128:] + relay_l[:, block(i)].astype(F32)).astype(BF)
    o_copies[3].start()
    o_copies[2].wait_recv()
    o_copies[3].wait_recv()
    total_down = jnp.zeros((256, 1024), F32)
    for i in range(4):
        value = part(tp, i) + latent[:, columns(tp, i)].astype(F32)
        value = value + arr_r[:, block(i)].astype(F32) + arr_l[:, block(i)].astype(F32)
        lat_out[:, block(i)] = value.astype(BF)
    for i in range(4):
        down = w[:, :, pl.ds(1536 + 64 * i, 64), :].reshape(1024, 256)
        total_down = total_down + nt(lat_out[:, block(i)], down)
    for t in range(4):
        downs[t] = total_down[64 * t : 64 * t + 64].astype(BF)
    third = scatter(downs, down_in, d_send, d_recv)
    for c in third:
        c.start()
    down_in[pl.ds(tp, 1)] = downs[pl.ds(tp, 1)]
    for c in third:
        c.wait_recv()
    sums = down_in[0].astype(F32) + down_in[1].astype(F32) + down_in[2].astype(F32) + down_in[3].astype(F32)
    down_share[...] = sums.astype(BF)
    fourth = spread(down_share, patch, e_send, e_recv)
    for c in fourth:
        c.start()
    patch[pl.ds(tp, 1)] = down_share[...][None]
    for c in fourth:
        c.wait_recv()
    patch_out = patch[...].reshape(256, 1024)
    final = (iota((16, 256), 1) == group_one - 1.0).astype(BF)
    trail[...] = dot(final, patch_out).astype(BF)
    trail_copy = remote(trail, trail_in, trail_send, trail_recv, next_first)

    @pl.when(tp == 3)
    def _():
        trail_copy.start()

    result = hidden[...].astype(F32) + dot((c256 == slot_col).astype(BF), patch_out)
    out[...] = result.astype(BF)

    @pl.when(tp == 0)
    def _():
        trail_copy.wait_recv()
        row = trail_in[...][0:1].astype(F32)
        out[...] = (out[...].astype(F32) + jnp.where(run_col == 0.0, row, F32(0.0))).astype(BF)

    @pl.when(tp == 3)
    def _():
        trail_copy.wait_send()

    @pl.when(tp == 0)
    def _():
        for c in leads:
            c.wait_send()

    for c in first + second + third + fourth + z_copies + o_copies:
        c.wait_send()
    for i in range(4):
        for c in sent(i):
            c.wait_send()
        passed(i).wait_send()
    for group_of in sets:
        for c in group_of:
            c.wait_send()


def second_stage(hidden, marks_row, marks_col, counts, gain, weights):
    anywhere = pl.BlockSpec(memory_space=pl.ANY)
    vmem = pl.BlockSpec(memory_space=pltpu.VMEM)
    dma = pltpu.SemaphoreType.DMA

    def v(*shape, kind=BF):
        return pltpu.VMEM(shape, kind)

    return pl.pallas_call(
        second_kernel,
        out_shape=jax.ShapeDtypeStruct(hidden.shape, BF),
        in_specs=[vmem] * 5 + [anywhere],
        out_specs=vmem,
        scratch_shapes=[
            v(4, 4, ROWS, 256), v(256, 128), v(4, 64, 1152), v(4, 64, 1152), v(64, 1024), v(4, 64, 1024),
            v(256, 4096), v(256, 1, kind=F32), v(3, 256, 256, kind=F32), v(272, 256), v(4, 4, 272, 256),
            v(4, 256, 128), v(4, 256, 1, kind=F32), v(4, 256, 1, kind=F32), v(4, 256, 128, kind=F32), v(256, 512),
            v(256, 1024), v(128, 1024), v(128, 1024), v(256, 1024), v(256, 1024), v(256, 1024), v(256, 1024),
            v(256, 1024), v(4, 64, 1024), v(4, 64, 1024), v(64, 1024), v(4, 64, 1024),
            v(16, 1152, kind=F32), v(16, 1152, kind=F32), v(16, 1024), v(16, 1024),
            dma, dma((3,)), dma((3,)), dma((3,)), dma((3,)), dma((8,)), dma((8,)), dma((4,)), dma((4,)),
            dma((3,)), dma((3,)), dma((16,)), dma((16,)), dma((4,)), dma((4,)), dma((3,)), dma((3,)),
            dma((3,)), dma((3,)), dma((4,)), dma, dma, dma,
        ],
        compiler_params=pltpu.CompilerParams(collective_id=1, has_side_effects=True, vmem_limit_bytes=62 * 2**20),
    )(hidden, marks_row, marks_col, counts, gain, weights)


def local(
    byte_embed, patch_start, enc_gain, enc_qkv, enc_out, up_proj, lat_gain, query_proj, key_proj,
    value_matrix, out_proj, down_proj,
):
    local_count = jnp.sum(patch_start)
    whole, hidden, counts = first_stage(
        up_proj, query_proj, key_proj, value_matrix, out_proj, down_proj.T, byte_embed,
        jnp.full((8, 128), local_count, jnp.int32), enc_gain[None, :], enc_qkv, enc_out,
    )
    marks = patch_start.astype(BF)
    marks_row = jnp.broadcast_to(marks[None, :], (16, 256))
    marks_col = jnp.broadcast_to(marks[:, None], (256, 128))
    return second_stage(hidden, marks_row, marks_col, counts, lat_gain[None, :], whole)


def solution(mesh):
    placed = (
        P(("dp", "ctx", "tp"), None), P(("dp", "ctx", "tp")), P(), P(), P(), P("ctx", "tp"), P(),
        P("ctx", "tp"), P("ctx", "tp"), P("ctx", "tp"), P("tp", "ctx"), P("tp", "ctx"),
    )
    return jax.shard_map(
        local, mesh=mesh, in_specs=placed, out_specs=P(("dp", "ctx", "tp"), None), check_vma=False
    )
```

profile of v0, /device:TPU:32, one launch (start us, length us, event | category | flops | bytes accessed | tf_op | source)
XLA Modules:
  0.0 231.6 jit_solution(4594916980718963385)
XLA Ops:
  0.0 1.4 fusion
  1.4 1.2 broadcast_in_dim.10.count
  2.6 0.6 broadcast_in_dim.23.marks_row
  3.2 0.7 broadcast_in_dim.24.marks_col
  4.0 86.3 %shard_map.118 = (bf16[4,4,1792,256]{3,2,1,0:T(8,128)(2,1)}, bf16[256,1024]{1,0:T(8,128)(2,1)}, s32[4,8,128]{2,1,0:T(8,128)}) custom-call(bf16[64,1024]{1,0:T(8,128)(2,1)} %up.1, bf16[256,512]{1,0:T(8,128)(2,1)} %query_w.1, bf16[256,128]{1,0:T(8,128)(2,1)} %key_w.1, bf16[256,128]{1,0:T(8,128)(2,1)} %value_w.1, bf16[512,256]{1,0:T(8,128)(2,1)} %out_w.1, ...), custom_call_target="tpu_custom_call" | custom-call | tf_op jit(solution)/shard_map/pallas_call | solution.py:383
  90.3 139.5 %shard_map.119 = bf16[256,1024]{1,0:T(8,128)(2,1)} custom-call(bf16[256,1024]{1,0:T(8,128)(2,1)} %get-tuple-element.8.hidden, bf16[16,256]{1,0:T(8,128)(2,1)} %broadcast_in_dim.23.marks_row, bf16[256,128]{1,0:T(8,128)(2,1)} %broadcast_in_dim.24.marks_col, s32[4,8,128]{2,1,0:T(8,128)} %get-tuple-element.9.counts, f32[1,4096]{1,0:T(1,128)} %bitcast.4, ...), custom_call_target="tpu_custom_call" | custom-call | tf_op jit(solution)/shard_map/pallas_call | solution.py:740
  229.7 1.9 copy.14
where the time goes:
time: 232 us
  Pallas kernels  226 us (97%)
  local copies, waits for them, and re-layouts  4.44 us (2%)
    pallas_call x1, Pallas kernels, second_stage(): pl.pallas_call(second_kernel, out_shape=jax.ShapeDtypeStruct(hidden.shape...  139 us
    pallas_call x1, Pallas kernels, first_stage(): pl.pallas_call(first_kernel, out_shape=(jax.ShapeDtypeStruct((4, 4, ROWS,...  86.3 us

commit v1 on v0

--- a/solution.py
+++ b/solution.py
@@ -15,13 +15,11 @@
 MESH = pl.DeviceIdType.MESH
 BF = jnp.bfloat16
 F32 = jnp.float32
-ROWS = 1792
-HALF = ROWS // 2
-A_ROWS = 448
-
-
-def gather_plan(rate=46.6e3, latency=2.0):
-    sizes = {"A": A_ROWS, "B": HALF - A_ROWS}
+FIRST, SECOND = 1024, 768
+
+
+def gather_plan(whole_rows, rate=46.6e3, latency=2.0):
+    sizes = {"A": whole_rows // 4, "B": whole_rows // 4}
     free = {link: 0.0 for link in ("E", "I", "X+", "X-", "D")}
     heap, order, sends, halves = [], [], [], {}
 
@@ -66,7 +64,7 @@
     first = []
     have(0.0, "A", 0, 0, first)
     have(0.0, "B", 0, 0, first)
-    order.append((None, first))
+    order.append((0.0, None, first))
     while heap:
         now, k = heapq.heappop(heap)
         kind, dz, dx, half, link = sends[k]
@@ -89,11 +87,11 @@
                     send(now, kind, 2, dx, "mine", "I", batch)
                 if halves[key] == 2:
                     have(now, kind, dz, dx, batch)
-        order.append((k, batch))
+        order.append((now, k, batch))
     return order, sends
 
 
-ORDER, SENDS = gather_plan()
+PLANS = {FIRST: gather_plan(FIRST), SECOND: gather_plan(SECOND, 38e3, 2.5)}
 
 
 def enter(devices):
@@ -113,32 +111,72 @@
     )
 
 
-def normal(rows, gain):
-    floats = rows.astype(F32)
-    return (floats * lax.rsqrt(jnp.mean(floats * floats, axis=-1, keepdims=True) + EPS) * gain).astype(BF)
-
-
-def nt(a, b):
-    return lax.dot_general(a, b, (((1,), (1,)), ((), ())), preferred_element_type=F32)
-
-
-def first_kernel(
-    up, query_w, key_w, value_w, out_w, down_t, embed, count, gain, qkv_hbm, out_hbm,
-    whole, hidden, counts,
-    own, halo, relay, qkv, enc_out, normed, query, keyval, mixed, bias,
-    own_sem, w_sem, g_send, g_recv, h_send, h_recv, r_send, r_recv, x_send, x_recv, c_send, c_recv,
-):
-    ctx, tp, dp = position()
+def gather_links(ctx, tp, dp):
     h, x, lo, core = ctx // 4, ctx % 4, dp // 2, dp % 2
     way = 2 * lo - 1
     turned = (1 - lo) * 2 + core
-    link = {
+    return {
         "E": (((h + way + 4) % 4) * 4 + x, tp, turned),
         "I": (ctx, tp, turned),
         "X+": (h * 4 + (x + 1) % 4, tp, dp),
         "X-": (h * 4 + (x + 3) % 4, tp, dp),
         "D": (ctx, tp, lo * 2 + 1 - core),
     }
+
+
+class Gather:
+    def __init__(self, own, whole, send, recv):
+        self.own, self.whole, self.send, self.recv = own, whole, send, recv
+        self.order, self.sends = PLANS[own.shape[0]]
+        self.at = 0
+
+    def copy(self, k):
+        ctx, tp, dp = position()
+        h, x, lo, core = ctx // 4, ctx % 4, dp // 2, dp % 2
+        kind, dz, dx, half, where = self.sends[k]
+        rows = self.own.shape[0] // 4
+        base = core * 2 * rows + (0 if kind == "A" else rows)
+        if half is not None:
+            rows = rows // 2
+            base = base + {"mine": lo, "other": 1 - lo}.get(half, half) * rows
+        part = pl.ds(pl.multiple_of(base, 16), rows)
+        piece = self.whole.at[(h + dz * (2 * lo - 1) + 8) % 4, (x + dx + 4) % 4, part]
+        device = gather_links(ctx, tp, dp)[where]
+        src = self.own.at[part] if (dz, dx) == (0, 0) else piece
+        return remote(src, piece, self.send.at[k], self.recv.at[k], device)
+
+    def until(self, time):
+        while self.at < len(self.order) and self.order[self.at][0] <= time:
+            _, k, batch = self.order[self.at]
+            if k is not None:
+                self.copy(k).wait_recv()
+            for s in batch:
+                self.copy(s).start()
+            self.at += 1
+
+    def drain(self):
+        for k in range(len(self.sends)):
+            self.copy(k).wait_send()
+
+
+def normal(rows, gain):
+    floats = rows.astype(F32)
+    return (floats * lax.rsqrt(jnp.mean(floats * floats, axis=-1, keepdims=True) + EPS) * gain).astype(BF)
+
+
+def nt(a, b):
+    return lax.dot_general(a, b, (((1,), (1,)), ((), ())), preferred_element_type=F32)
+
+
+def first_kernel(
+    up, query_w, key_w, value_w, embed, count, gain, qkv_hbm, out_hbm,
+    whole, hidden, counts,
+    own, halo, relay, qkv, enc_out, normed, query, keyval, mixed, bias, peaks_of, totals_of, sums_of,
+    own_sem, w_sem, g_send, g_recv, h_send, h_recv, r_send, r_recv, x_send, x_recv, c_send, c_recv,
+):
+    ctx, tp, dp = position()
+    h, x = ctx // 4, ctx % 4
+    link = gather_links(ctx, tp, dp)
     loads = [pltpu.make_async_copy(up.at[:, pl.ds(256 * i, 256)], own.at[pl.ds(64 * i, 64)], own_sem.at[i]) for i in range(4)]
     loads += [
         pltpu.make_async_copy(query_w.at[:, pl.ds(256 * i, 256)], own.at[pl.ds(256 + 256 * i, 256)], own_sem.at[4 + i])
@@ -146,28 +184,13 @@
     ]
     loads.append(pltpu.make_async_copy(key_w, own.at[pl.ds(768, 256), pl.ds(0, 128)], own_sem.at[6]))
     loads.append(pltpu.make_async_copy(value_w, own.at[pl.ds(768, 256), pl.ds(128, 128)], own_sem.at[7]))
-    loads.append(pltpu.make_async_copy(out_w, own.at[pl.ds(1024, 512)], own_sem.at[8]))
-    loads += [
-        pltpu.make_async_copy(down_t.at[:, pl.ds(256 * i, 256)], own.at[pl.ds(1536 + 64 * i, 64)], own_sem.at[9 + i])
-        for i in range(4)
-    ]
     for load in loads:
         load.start()
     weights = [pltpu.make_async_copy(qkv_hbm, qkv, w_sem.at[0]), pltpu.make_async_copy(out_hbm, enc_out, w_sem.at[1])]
     for load in weights:
         load.start()
 
-    def copy(k):
-        kind, dz, dx, half, where = SENDS[k]
-        rows = A_ROWS if kind == "A" else HALF - A_ROWS
-        base = core * HALF + (0 if kind == "A" else A_ROWS)
-        if half is not None:
-            rows = rows // 2
-            base = base + {"mine": lo, "other": 1 - lo}.get(half, half) * rows
-        part = pl.ds(pl.multiple_of(base, 16), rows)
-        piece = whole.at[(h + dz * way + 8) % 4, (x + dx + 4) % 4, part]
-        return remote(own.at[part] if (dz, dx) == (0, 0) else piece, piece, g_send.at[k], g_recv.at[k], link[where])
-
+    gather = Gather(own, whole, g_send, g_recv)
     last = (tp == 3).astype(jnp.int32)
     zero = (tp == 0).astype(jnp.int32)
     following = ((ctx + last) % 16, (tp + 1) % 4, dp)
@@ -240,8 +263,7 @@
     def first_sends():
         for load in loads:
             load.wait()
-        for s in ORDER[0][1]:
-            copy(s).start()
+        gather.until(0.0)
 
     def project(block, rows, columns):
         normed[...] = normal(rows, gain[...])
@@ -308,19 +330,44 @@
 
     lanes = lax.broadcasted_iota(jnp.int32, (256, 128), 1)
 
-    def attend(pair):
-        at = pl.ds(128 * pair, 128)
+    def attend(block, pair, carry):
+        at = pl.ds(pl.multiple_of(128 * pair, 128), 128)
+        rows = pl.ds(256 * block, 256)
         both = query[:, at]
-        k = keyval[:, at]
-        v = keyval[:, pl.ds(1024 + 128 * pair, 128)]
-        outs = []
+        k = keyval[rows, at]
+        v = keyval[rows, pl.ds(pl.multiple_of(1024 + 128 * pair, 128), 128)]
+        peaks, totals, outs, fades = [], [], [], []
         for side in range(2):
             q = jnp.where((lanes < 64) == (side == 0), both, jnp.zeros_like(both))
-            s = nt(q, k) + bias[...]
-            e = jnp.exp(s - jnp.max(s, axis=-1, keepdims=True))
-            total = jnp.sum(e, axis=-1, keepdims=True)
-            outs.append(jnp.dot(e.astype(BF), v, preferred_element_type=F32) / total)
-        mixed[:, at] = jnp.where(lanes < 64, outs[0], outs[1]).astype(BF)
+            s = nt(q, k) + bias[:, rows]
+            peak = jnp.max(s, axis=-1, keepdims=True)
+            if block != 2:
+                old = peaks_of[:, at][:, 64 * side : 64 * side + 1]
+                peak = jnp.maximum(peak, old)
+                fades.append(jnp.exp(old - peak))
+            e = jnp.exp(s - peak)
+            peaks.append(peak)
+            totals.append(jnp.sum(e, axis=-1, keepdims=True))
+            outs.append(jnp.dot(e.astype(BF), v, preferred_element_type=F32))
+        first = lanes < 64
+        total, out = jnp.where(first, *totals), jnp.where(first, *outs)
+        if block != 2:
+            fade = jnp.where(first, *fades)
+            total = total + totals_of[:, at] * fade
+            out = out + sums_of[:, at] * fade
+        if block == 0:
+            mixed[:, at] = (out / total).astype(BF)
+        else:
+            peaks_of[:, at] = jnp.where(first, *peaks)
+            totals_of[:, at] = total
+            sums_of[:, at] = out
+        return carry
+
+    def attend_block(block, times):
+        for i, time in enumerate(times):
+            n = 8 // len(times)
+            lax.fori_loop(n * i, n * i + n, lambda pair, carry: attend(block, pair, carry), 0)
+            gather.until(time)
 
     def finish():
         weights[1].wait()
@@ -333,26 +380,20 @@
 
         lax.fori_loop(0, 4, tile, 0)
 
-    jobs = {0: [own_part], 3: [relay_part], 14: [near_part], FAR: [far_part]}
-    for pair in range(8):
-        jobs.setdefault(FAR + 2 + 2 * pair, []).append(lambda pair=pair: attend(pair))
-    jobs.setdefault(FAR + 18, []).append(finish)
+    own_part()
+    relay_part()
     first_sends()
     keep = pltpu.make_async_copy(own, whole.at[h, x], w_sem.at[2])
     keep.start()
-    done = []
-    for step, (k, batch) in enumerate(ORDER):
-        if step > 0:
-            copy(k).wait_recv()
-            for s in batch:
-                copy(s).start()
-        for job in jobs.get(step, []):
-            job()
-            done.append(job)
-    for step in sorted(jobs):
-        for job in jobs[step]:
-            if job not in done:
-                job()
+    attend_block(2, (2.0, 4.0, 6.0, 8.0))
+    near_part()
+    gather.until(10.0)
+    attend_block(1, (13.0, 16.0, 19.0, 22.0))
+    far_part()
+    gather.until(26.0)
+    attend_block(0, (28.0, 30.0, 33.0, 36.0))
+    finish()
+    gather.until(1000.0)
     keep.wait()
 
     @pl.when(jnp.logical_not(crossing))
@@ -368,29 +409,25 @@
     each_over(lambda c: c.wait_send(), (0, 1, 2, 3))
     for i, device in enumerate(tps):
         remote(count, counts.at[tp], c_send.at[i], c_recv.at[i], device).wait()
-    for k in range(len(SENDS)):
-        copy(k).wait_send()
-
-
-FAR = 46
-
-
-def first_stage(up, query_w, key_w, value_w, out_w, down_t, embed, count, gain, qkv, enc_out):
+    gather.drain()
+
+
+def first_stage(up, query_w, key_w, value_w, embed, count, gain, qkv, enc_out):
     anywhere = pl.BlockSpec(memory_space=pl.ANY)
     vmem = pl.BlockSpec(memory_space=pltpu.VMEM)
-    n = len(SENDS)
+    n = len(PLANS[FIRST][1])
     dma = pltpu.SemaphoreType.DMA
     return pl.pallas_call(
         first_kernel,
         out_shape=(
-            jax.ShapeDtypeStruct((4, 4, ROWS, 256), BF),
+            jax.ShapeDtypeStruct((4, 4, FIRST, 256), BF),
             jax.ShapeDtypeStruct(embed.shape, BF),
             jax.ShapeDtypeStruct((4, 8, 128), jnp.int32),
         ),
-        in_specs=[anywhere] * 6 + [vmem] * 3 + [anywhere] * 2,
+        in_specs=[anywhere] * 4 + [vmem] * 3 + [anywhere] * 2,
         out_specs=(anywhere, vmem, vmem),
         scratch_shapes=[
-            pltpu.VMEM((ROWS, 256), BF),
+            pltpu.VMEM((FIRST, 256), BF),
             pltpu.VMEM((2, 256, 1024), BF),
             pltpu.VMEM((64, 1024), BF),
             pltpu.VMEM((1024, 3072), BF),
@@ -400,29 +437,42 @@
             pltpu.VMEM((768, 2048), BF),
             pltpu.VMEM((256, 1024), BF),
             pltpu.VMEM((256, 768), F32),
-            dma((13,)), dma((3,)), dma((n,)), dma((n,)), dma((2,)), dma((2,)), dma((3,)), dma, dma, dma((8,)),
+            pltpu.VMEM((256, 1024), F32),
+            pltpu.VMEM((256, 1024), F32),
+            pltpu.VMEM((256, 1024), F32),
+            dma((8,)), dma((3,)), dma((n,)), dma((n,)), dma((2,)), dma((2,)), dma((3,)), dma, dma, dma((8,)),
             dma((3,)), dma((3,)),
         ],
         compiler_params=pltpu.CompilerParams(collective_id=0, has_side_effects=True, vmem_limit_bytes=62 * 2**20),
-    )(up, query_w, key_w, value_w, out_w, down_t, embed, count, gain, qkv, enc_out)
+    )(up, query_w, key_w, value_w, embed, count, gain, qkv, enc_out)
 
 
 def second_kernel(
-    hidden, marks_row, marks_col, counts, gain, weights_hbm,
+    hidden, marks_row, marks_col, counts, gain, weights_hbm, out_w, down_t,
     out,
-    w, ones, parts, arrived, share, pooled, latent, scaled, acc, kv, kv_all, query, mx, tot, mix, attn,
-    far, relay_r, relay_l, to_right, to_left, arr_r, arr_l, lat_out, downs, down_in, down_share, patch,
+    w, own, w2, ones, parts, part_relay, arrived, share, pooled, latent, scaled, acc, kv, kv_all, query, mx, tot, mix, attn,
+    far, relay_r, relay_l, to_right, to_left, arr_r, arr_l, lat_out, downs, down_relay, down_in, down_share, patch,
     lead, lead_in, trail, trail_in,
     w_sem, p_send, p_recv, s_send, s_recv, l_send, l_recv, f_send, f_recv, z_send, z_recv, x_send, x_recv,
     o_send, o_recv, d_send, d_recv, e_send, e_recv, lead_send, lead_recv, trail_send, trail_recv,
+    own_sem, g_send, g_recv,
 ):
     ctx, tp, dp = position()
     h, x = ctx // 4, ctx % 4
     load = pltpu.make_async_copy(weights_hbm, w, w_sem)
     load.start()
+    loads = [pltpu.make_async_copy(out_w, own.at[pl.ds(0, 512)], own_sem.at[0])]
+    loads += [
+        pltpu.make_async_copy(down_t.at[:, pl.ds(256 * i, 256)], own.at[pl.ds(512 + 64 * i, 64)], own_sem.at[1 + i])
+        for i in range(4)
+    ]
+    for c in loads:
+        c.start()
+    gather = Gather(own, w2, g_send, g_recv)
+    link = gather_links(ctx, tp, dp)
     tps = [(ctx, (tp + i) % 4, dp) for i in (1, 2, 3)]
     up_y, down_y = tps[0], tps[2]
-    zs = [(((h + i) % 4) * 4 + x, tp, dp) for i in (1, 3, 2)]
+    zs = [(((h + i) % 4) * 4 + x, tp, dp) for i in (1, 3)]
     right, left = (h * 4 + (x + 1) % 4, tp, dp), (h * 4 + (x + 3) % 4, tp, dp)
     next_first = ((ctx + 1) % 16, tp * 0, dp)
     before_all = [((ctx + 15) % 16, t, dp) for t in range(4)]
@@ -432,7 +482,7 @@
         for device in devices:
             pl.semaphore_signal(barrier, inc=1, device_id=device, device_id_type=MESH)
 
-    greet(tps + zs + [right, left, next_first])
+    greet(tps + zs + [right, left, next_first] + [link[name] for name in ("E", "I", "D")])
 
     @pl.when(tp == 0)
     def _():
@@ -466,39 +516,76 @@
     lead[:, pl.ds(0, 1024)] = dot(leading, hidden[...])
     lead[:, pl.ds(1024, 128)] = dot(leading, ones[...])
 
-    pl.semaphore_wait(barrier, 9 + 4 * (tp == 0).astype(jnp.int32))
-
-    leads = [remote(lead, lead_in, lead_send.at[t], lead_recv, before_all[t]) for t in range(4)]
+    pl.semaphore_wait(barrier, 11 + 4 * (tp == 0).astype(jnp.int32))
+
+    leads = [remote(lead.at[pl.ds(0, 8)], lead_in, lead_send.at[t], lead_recv, before_all[t]) for t in range(4)]
 
     @pl.when(tp == 0)
     def _():
         for c in leads:
             c.start()
 
-    def scatter(src, dst, send, recv):
-        return [remote(src.at[(tp + i + 1) % 4], dst.at[tp], send.at[i], recv.at[i], tps[i]) for i in range(3)]
+    opposite, above, below = (tp + 2) % 4, (tp + 1) % 4, (tp + 3) % 4
+    half_a, half_b = pl.ds(0, 32), pl.ds(32, 32)
+
+    def scatter(src, relay, dst, send, recv):
+        return [
+            remote(src.at[opposite, half_a], relay.at[0], send.at[0], recv.at[0], up_y),
+            remote(src.at[opposite, half_b], relay.at[1], send.at[1], recv.at[1], down_y),
+            remote(src.at[above], dst.at[0], send.at[2], recv.at[2], up_y),
+            remote(src.at[below], dst.at[1], send.at[3], recv.at[3], down_y),
+        ]
+
+    def pass_on(src, relay, copies):
+        copies[0].wait_recv()
+        src[above, half_a] = (src[above, half_a].astype(F32) + relay[0].astype(F32)).astype(BF)
+        copies[2].start()
+        copies[1].wait_recv()
+        src[below, half_b] = (src[below, half_b].astype(F32) + relay[1].astype(F32)).astype(BF)
+        copies[3].start()
+
+    def gathered(src, dst, copies):
+        copies[2].wait_recv()
+        copies[3].wait_recv()
+        return src[tp].astype(F32) + dst[0].astype(F32) + dst[1].astype(F32)
 
     def spread(src, dst, send, recv):
-        return [remote(src, dst.at[tp], send.at[i], recv.at[i], tps[i]) for i in range(3)]
-
-    first = scatter(parts, arrived, p_send, p_recv)
-    for c in first:
+        lower, upper = dst.at[below, half_a], dst.at[above, half_b]
+        return [
+            remote(src, dst.at[tp], send.at[0], recv.at[0], up_y),
+            remote(src, dst.at[tp], send.at[1], recv.at[1], down_y),
+            remote(lower, lower, send.at[2], recv.at[2], up_y),
+            remote(upper, upper, send.at[3], recv.at[3], down_y),
+        ]
+
+    def spread_rest(copies):
+        for i in (0, 1):
+            copies[i].wait_recv()
+            copies[2 + i].start()
+        for i in (2, 3):
+            copies[i].wait_recv()
+
+    first = scatter(parts, part_relay, arrived, p_send, p_recv)
+    for c in first[:2]:
         c.start()
-    arrived[pl.ds(tp, 1)] = parts[pl.ds(tp, 1)]
-    for c in first:
-        c.wait_recv()
+    for c in loads:
+        c.wait()
+    gather.until(0.0)
+    w2[pl.ds(h, 1), pl.ds(x, 1)] = own[...][None, None]
+    pass_on(parts, part_relay, first)
+    gather.until(7.0)
+    sums = gathered(parts, arrived, first)
     leads[0].wait_recv()
-    sums = arrived[0].astype(F32) + arrived[1].astype(F32) + arrived[2].astype(F32) + arrived[3].astype(F32)
     my_row = iota((64, 1152), 0) + (64 * tp).astype(F32)
     sums = sums + jnp.where(my_row == group_one - 1.0, lead_in[0:1], F32(0.0))
     share[...] = (sums[:, :1024] / jnp.maximum(sums[:, 1024:1025], 1.0)).astype(BF)
     second = spread(share, pooled, s_send, s_recv)
-    for c in second:
+    for c in second[:2]:
         c.start()
     pooled[pl.ds(tp, 1)] = share[...][None]
     load.wait()
-    for c in second:
-        c.wait_recv()
+    gather.until(14.0)
+    spread_rest(second)
 
     def columns(t, i):
         return pl.ds(pl.multiple_of(1024 * t + 256 * i, 256), 256)
@@ -520,6 +607,7 @@
         latent[:, columns(tp, i)] = dot(all_pooled, block).astype(BF)
         for c in sent(i):
             c.start()
+    gather.until(18.0)
 
     def contract(t, i, fresh=False):
         values = latent[:, columns(t, i)].astype(F32)
@@ -532,6 +620,7 @@
 
     for i in range(4):
         contract(tp, i, i == 0)
+        gather.until(19.5 + 1.5 * i)
     for i in range(4):
         remote(latent.at[:, columns(tp, i)], latent.at[:, columns(tp, i)], l_send.at[i], l_recv.at[i], up_y).wait_recv()
         if i < 2:
@@ -541,15 +630,21 @@
             passed(i).start()
         contract((tp + 3) % 4, i)
         contract((tp + 1) % 4, i)
+        gather.until(26.0 + 2.0 * i)
     for i in (0, 2, 1, 3):
         passed(i).wait_recv()
         contract((tp + 2) % 4, i)
+    gather.until(35.0)
     scale = lax.rsqrt(scaled[...] * F32(1.0 / 4096.0) + EPS)
     kv[pl.ds(0, 256)] = (acc[2] * scale).astype(BF)
     kv[pl.ds(256, 16)] = jnp.broadcast_to(group_one, (16, 256)).astype(BF)
 
-    z_copies = [remote(kv, kv_all.at[h, x], z_send.at[i], z_recv.at[i], zs[i]) for i in range(3)]
-    for c in z_copies:
+    low_rows, high_rows = pl.ds(0, 128), pl.ds(128, 144)
+    z_low, z_high = kv_all.at[(h + 3) % 4, x, low_rows], kv_all.at[(h + 1) % 4, x, high_rows]
+    z_copies = [remote(kv, kv_all.at[h, x], z_send.at[i], z_recv.at[i], zs[i]) for i in range(2)]
+    z_copies.append(remote(z_low, z_low, z_send.at[2], z_recv.at[2], zs[0]))
+    z_copies.append(remote(z_high, z_high, z_send.at[3], z_recv.at[3], zs[1]))
+    for c in z_copies[:2]:
         c.start()
 
     def across(j, dz):
@@ -571,7 +666,7 @@
     kv_all[pl.ds(h, 1), pl.ds(x, 1)] = kv[...][None, None]
     for head in range(4):
         q = acc[head // 2][:, 128 * (head % 2) : 128 * (head % 2) + 128] * scale
-        query[head] = q.astype(BF)
+        query[pl.ds(256 * head, 256)] = q.astype(BF)
 
     shrink = F32(1.0) / jnp.sqrt(F32(HEAD_SIZE))
 
@@ -584,62 +679,80 @@
             keys = kv_all[z, xx, pl.ds(0, 256), pl.ds(0, 128)]
             values = kv_all[z, xx, pl.ds(0, 256), pl.ds(128, 128)]
             limit = kv_all[z, xx, pl.ds(256, 16), :][0:1].astype(F32)
-            allowed = c256 < limit
+            bias = jnp.where(c256[0:1] < limit, F32(0.0), F32(-1e30))
             if fresh:
-                allowed = allowed & (c256 <= r256)
-            bias = jnp.where(allowed, F32(0.0), F32(-1e30))
-
-            def one_head(head, carry):
-                s = nt(query[head], keys) * shrink + bias
+                causal = jnp.where(c256 <= r256, F32(0.0), F32(-1e30))
+                bias = bias + jnp.concatenate([causal, causal], axis=0)
+
+            def two_heads(i, carry):
+                rows = pl.ds(pl.multiple_of(512 * i, 512), 512)
+                s = nt(query[rows], keys) * shrink + bias
                 peak = jnp.max(s, axis=-1, keepdims=True)
                 if not fresh:
-                    old = mx[head]
+                    old = mx[rows]
                     peak = jnp.maximum(peak, old)
                 e = jnp.exp(s - peak)
                 total = jnp.sum(e, axis=-1, keepdims=True)
                 mixed = dot(e.astype(BF), values)
                 if not fresh:
                     fade = jnp.exp(old - peak)
-                    total = total + tot[head] * fade
-                    mixed = mixed + mix[head] * fade
-                mx[head] = peak
-                tot[head] = total
-                mix[head] = mixed
+                    total = total + tot[rows] * fade
+                    mixed = mixed + mix[rows] * fade
+                mx[rows] = peak
+                tot[rows] = total
+                mix[rows] = mixed
                 return carry
 
-            lax.fori_loop(0, 4, one_head, 0)
+            lax.fori_loop(0, 2, two_heads, 0)
+
+    def along(j):
+        sets[j][0].start()
+        sets[j][1].start()
+
+    def turn(j):
+        for i in (0, 1):
+            sets[j][i].wait_recv()
+            sets[j][i + 2].start()
 
     attend(0, 0, True)
-    for j in range(4):
-        if j > 0:
-            z_copies[j - 1].wait_recv()
-            sets[j][0].start()
-            sets[j][1].start()
-            for i in (0, 1):
-                sets[j - 1][i].wait_recv()
-                sets[j - 1][i + 2].start()
-            attend(turns[j], 0)
-            attend(turns[j - 1], 3)
-            attend(turns[j - 1], 1)
+    gather.until(38.0)
     for i in (0, 1):
-        sets[3][i].wait_recv()
-        sets[3][i + 2].start()
-    attend(turns[3], 3)
-    attend(turns[3], 1)
+        z_copies[i].wait_recv()
+        z_copies[i + 2].start()
+        along(i + 1)
+    turn(0)
+    attend(3, 0)
+    attend(1, 0)
+    attend(0, 3)
+    z_copies[2].wait_recv()
+    z_copies[3].wait_recv()
+    along(3)
+    attend(0, 1)
+    turn(1)
+    gather.until(1000.0)
+    attend(3, 3)
+    turn(2)
+    attend(3, 1)
+    attend(2, 0)
+    attend(1, 3)
+    turn(3)
+    attend(1, 1)
+    attend(2, 3)
+    attend(2, 1)
     for j in range(4):
         for i in (2, 3):
             sets[j][i].wait_recv()
         attend(turns[j], 2)
     for head in range(4):
-        attn[:, pl.ds(128 * head, 128)] = (mix[head] / tot[head]).astype(BF)
+        rows = pl.ds(256 * head, 256)
+        attn[:, pl.ds(128 * head, 128)] = (mix[rows] / tot[rows]).astype(BF)
 
     def part(t, i):
-        return dot(attn[...], w[t, i, pl.ds(1024, 512), :])
+        return dot(attn[...], w2[t, i, pl.ds(0, 512), :])
 
     def block(i):
         return pl.ds(256 * i, 256)
 
-    opposite, above, below = (tp + 2) % 4, (tp + 1) % 4, (tp + 3) % 4
     low, high = pl.ds(0, 128), pl.ds(128, 128)
     for i in range(4):
         far[:, block(i)] = part(opposite, i).astype(BF)
@@ -673,45 +786,43 @@
         value = value + arr_r[:, block(i)].astype(F32) + arr_l[:, block(i)].astype(F32)
         lat_out[:, block(i)] = value.astype(BF)
     for i in range(4):
-        down = w[:, :, pl.ds(1536 + 64 * i, 64), :].reshape(1024, 256)
+        down = w2[:, :, pl.ds(512 + 64 * i, 64), :].reshape(1024, 256)
         total_down = total_down + nt(lat_out[:, block(i)], down)
     for t in range(4):
         downs[t] = total_down[64 * t : 64 * t + 64].astype(BF)
-    third = scatter(downs, down_in, d_send, d_recv)
-    for c in third:
+    third = scatter(downs, down_relay, down_in, d_send, d_recv)
+    for c in third[:2]:
         c.start()
-    down_in[pl.ds(tp, 1)] = downs[pl.ds(tp, 1)]
-    for c in third:
-        c.wait_recv()
-    sums = down_in[0].astype(F32) + down_in[1].astype(F32) + down_in[2].astype(F32) + down_in[3].astype(F32)
+    pass_on(downs, down_relay, third)
+    sums = gathered(downs, down_in, third)
     down_share[...] = sums.astype(BF)
+    final = (iota((16, 64), 1) + (64 * tp).astype(F32) == group_one - 1.0).astype(BF)
+    trail[...] = dot(final, down_share[...]).astype(BF)
     fourth = spread(down_share, patch, e_send, e_recv)
-    for c in fourth:
+    for c in fourth[:2]:
         c.start()
+    trail_copies = [remote(trail, trail_in.at[t], trail_send, trail_recv.at[t], next_first) for t in range(4)]
+    for t in range(4):
+
+        @pl.when(tp == t)
+        def _():
+            trail_copies[t].start()
+
     patch[pl.ds(tp, 1)] = down_share[...][None]
-    for c in fourth:
-        c.wait_recv()
+    spread_rest(fourth)
     patch_out = patch[...].reshape(256, 1024)
-    final = (iota((16, 256), 1) == group_one - 1.0).astype(BF)
-    trail[...] = dot(final, patch_out).astype(BF)
-    trail_copy = remote(trail, trail_in, trail_send, trail_recv, next_first)
-
-    @pl.when(tp == 3)
-    def _():
-        trail_copy.start()
-
     result = hidden[...].astype(F32) + dot((c256 == slot_col).astype(BF), patch_out)
     out[...] = result.astype(BF)
 
     @pl.when(tp == 0)
     def _():
-        trail_copy.wait_recv()
-        row = trail_in[...][0:1].astype(F32)
+        row = jnp.zeros((1, 1024), F32)
+        for t in range(4):
+            trail_copies[t].wait_recv()
+            row = row + trail_in[t][0:1].astype(F32)
         out[...] = (out[...].astype(F32) + jnp.where(run_col == 0.0, row, F32(0.0))).astype(BF)
 
-    @pl.when(tp == 3)
-    def _():
-        trail_copy.wait_send()
+    trail_copies[0].wait_send()
 
     @pl.when(tp == 0)
     def _():
@@ -727,34 +838,38 @@
     for group_of in sets:
         for c in group_of:
             c.wait_send()
-
-
-def second_stage(hidden, marks_row, marks_col, counts, gain, weights):
+    gather.drain()
+
+
+def second_stage(hidden, marks_row, marks_col, counts, gain, weights, out_w, down_t):
     anywhere = pl.BlockSpec(memory_space=pl.ANY)
     vmem = pl.BlockSpec(memory_space=pltpu.VMEM)
     dma = pltpu.SemaphoreType.DMA
 
+    n = len(PLANS[SECOND][1])
+
     def v(*shape, kind=BF):
         return pltpu.VMEM(shape, kind)
 
     return pl.pallas_call(
         second_kernel,
         out_shape=jax.ShapeDtypeStruct(hidden.shape, BF),
-        in_specs=[vmem] * 5 + [anywhere],
+        in_specs=[vmem] * 5 + [anywhere] * 3,
         out_specs=vmem,
         scratch_shapes=[
-            v(4, 4, ROWS, 256), v(256, 128), v(4, 64, 1152), v(4, 64, 1152), v(64, 1024), v(4, 64, 1024),
+            v(4, 4, FIRST, 256), v(SECOND, 256), v(4, 4, SECOND, 256), v(256, 128), v(4, 64, 1152), v(2, 32, 1152), v(2, 64, 1152), v(64, 1024), v(4, 64, 1024),
             v(256, 4096), v(256, 1, kind=F32), v(3, 256, 256, kind=F32), v(272, 256), v(4, 4, 272, 256),
-            v(4, 256, 128), v(4, 256, 1, kind=F32), v(4, 256, 1, kind=F32), v(4, 256, 128, kind=F32), v(256, 512),
+            v(1024, 128), v(1024, 1, kind=F32), v(1024, 1, kind=F32), v(1024, 128, kind=F32), v(256, 512),
             v(256, 1024), v(128, 1024), v(128, 1024), v(256, 1024), v(256, 1024), v(256, 1024), v(256, 1024),
-            v(256, 1024), v(4, 64, 1024), v(4, 64, 1024), v(64, 1024), v(4, 64, 1024),
-            v(16, 1152, kind=F32), v(16, 1152, kind=F32), v(16, 1024), v(16, 1024),
-            dma, dma((3,)), dma((3,)), dma((3,)), dma((3,)), dma((8,)), dma((8,)), dma((4,)), dma((4,)),
-            dma((3,)), dma((3,)), dma((16,)), dma((16,)), dma((4,)), dma((4,)), dma((3,)), dma((3,)),
-            dma((3,)), dma((3,)), dma((4,)), dma, dma, dma,
+            v(256, 1024), v(4, 64, 1024), v(2, 32, 1024), v(2, 64, 1024), v(64, 1024), v(4, 64, 1024),
+            v(16, 1152, kind=F32), v(8, 1152, kind=F32), v(16, 1024), v(4, 16, 1024),
+            dma, dma((4,)), dma((4,)), dma((4,)), dma((4,)), dma((8,)), dma((8,)), dma((4,)), dma((4,)),
+            dma((4,)), dma((4,)), dma((16,)), dma((16,)), dma((4,)), dma((4,)), dma((4,)), dma((4,)),
+            dma((4,)), dma((4,)), dma((4,)), dma, dma, dma((4,)),
+            dma((5,)), dma((n,)), dma((n,)),
         ],
         compiler_params=pltpu.CompilerParams(collective_id=1, has_side_effects=True, vmem_limit_bytes=62 * 2**20),
-    )(hidden, marks_row, marks_col, counts, gain, weights)
+    )(hidden, marks_row, marks_col, counts, gain, weights, out_w, down_t)
 
 
 def local(
@@ -763,13 +878,13 @@
 ):
     local_count = jnp.sum(patch_start)
     whole, hidden, counts = first_stage(
-        up_proj, query_proj, key_proj, value_matrix, out_proj, down_proj.T, byte_embed,
+        up_proj, query_proj, key_proj, value_matrix, byte_embed,
         jnp.full((8, 128), local_count, jnp.int32), enc_gain[None, :], enc_qkv, enc_out,
     )
     marks = patch_start.astype(BF)
     marks_row = jnp.broadcast_to(marks[None, :], (16, 256))
     marks_col = jnp.broadcast_to(marks[:, None], (256, 128))
-    return second_stage(hidden, marks_row, marks_col, counts, lat_gain[None, :], whole)
+    return second_stage(hidden, marks_row, marks_col, counts, lat_gain[None, :], whole, out_proj, down_proj.T)
 
 
 def solution(mesh):

time: 232 us -> 220 us (0.948)
  Pallas kernels: 226 us -> 214 us
    pallas_call x1, Pallas kernels: 86.3 us -> 70.7 us  [first_stage(): pl.pallas_call(first_kernel, out_shape=(jax.ShapeDtypeStruct((4, 4, FIRST...]
    pallas_call x1, Pallas kernels: 139 us -> 144 us  [second_stage(): pl.pallas_call(second_kernel, out_shape=jax.ShapeDtypeStruct(hidden.shape...]
where the time goes in v1:
time: 220 us
  Pallas kernels  214 us (97%)
  local copies, waits for them, and re-layouts  4.43 us (2%)
    pallas_call x1, Pallas kernels, second_stage(): pl.pallas_call(second_kernel, out_shape=jax.ShapeDtypeStruct(hidden.shape...  144 us
    pallas_call x1, Pallas kernels, first_stage(): pl.pallas_call(first_kernel, out_shape=(jax.ShapeDtypeStruct((4, 4, FIRST...  70.7 us

profile of v1, /device:TPU:32, one launch (start us, length us, event | category | flops | bytes accessed | tf_op | source)
XLA Modules:
  0.0 220.1 jit_solution(15817200684374429661)
XLA Ops:
  0.0 1.4 fusion
  1.4 1.2 broadcast_in_dim.10.count
  2.6 0.6 broadcast_in_dim.23.marks_row
  3.2 0.7 broadcast_in_dim.24.marks_col
  4.0 70.7 %shard_map.118 = (bf16[4,4,1024,256]{3,2,1,0:T(8,128)(2,1)}, bf16[256,1024]{1,0:T(8,128)(2,1)}, s32[4,8,128]{2,1,0:T(8,128)}) custom-call(bf16[64,1024]{1,0:T(8,128)(2,1)} %up.1, bf16[256,512]{1,0:T(8,128)(2,1)} %query_w.1, bf16[256,128]{1,0:T(8,128)(2,1)} %key_w.1, bf16[256,128]{1,0:T(8,128)(2,1)} %value_w.1, bf16[256,1024]{1,0:T(8,128)(2,1)} %embed.1, ...), custom_call_target="tpu_custom_call" | custom-call | tf_op jit(solution)/shard_map/pallas_call | solution.py:420
  74.6 143.6 %shard_map.119 = bf16[256,1024]{1,0:T(8,128)(2,1)} custom-call(bf16[256,1024]{1,0:T(8,128)(2,1)} %get-tuple-element.8.hidden, bf16[16,256]{1,0:T(8,128)(2,1)} %broadcast_in_dim.23.marks_row, bf16[256,128]{1,0:T(8,128)(2,1)} %broadcast_in_dim.24.marks_col, s32[4,8,128]{2,1,0:T(8,128)} %get-tuple-element.9.counts, f32[1,4096]{1,0:T(1,128)} %bitcast.4, ...), custom_call_target="tpu_custom_call" | custom-call | tf_op jit(solution)/shard_map/pallas_call | solution.py:854
  218.2 1.9 copy.14

commit v2 on v1

--- a/solution.py
+++ b/solution.py
@@ -670,16 +670,23 @@
 
     shrink = F32(1.0) / jnp.sqrt(F32(HEAD_SIZE))
 
-    def attend(dz, dx, fresh=False):
-        z, xx = (h + dz) % 4, (x + dx) % 4
-        other = z * 4 + xx
-
-        @pl.when(other <= ctx)
+    def attend(*chunks, fresh=False):
+        places = [((h + dz) % 4, (x + dx) % 4) for dz, dx in chunks]
+        seen = [z * 4 + xx <= ctx for z, xx in places]
+
+        @pl.when(seen[0] if len(chunks) == 1 else seen[0] | seen[1])
         def _():
-            keys = kv_all[z, xx, pl.ds(0, 256), pl.ds(0, 128)]
-            values = kv_all[z, xx, pl.ds(0, 256), pl.ds(128, 128)]
-            limit = kv_all[z, xx, pl.ds(256, 16), :][0:1].astype(F32)
-            bias = jnp.where(c256[0:1] < limit, F32(0.0), F32(-1e30))
+            joined, joined_v, biases = [], [], []
+            for (z, xx), reached in zip(places, seen):
+                joined.append(kv_all[z, xx, pl.ds(0, 256), pl.ds(0, 128)])
+                joined_v.append(kv_all[z, xx, pl.ds(0, 256), pl.ds(128, 128)])
+                limit = kv_all[z, xx, pl.ds(256, 16), :][0:1].astype(F32)
+                limit = jnp.where(reached, limit, F32(0.0))
+                biases.append(jnp.where(c256[0:1] < limit, F32(0.0), F32(-1e30)))
+            keys, values, bias = joined[0], joined_v[0], biases[0]
+            if len(chunks) == 2:
+                keys, values = jnp.concatenate(joined, axis=0), jnp.concatenate(joined_v, axis=0)
+                bias = jnp.concatenate(biases, axis=1)
             if fresh:
                 causal = jnp.where(c256 <= r256, F32(0.0), F32(-1e30))
                 bias = bias + jnp.concatenate([causal, causal], axis=0)
@@ -714,35 +721,31 @@
             sets[j][i].wait_recv()
             sets[j][i + 2].start()
 
-    attend(0, 0, True)
+    attend((0, 0), fresh=True)
     gather.until(38.0)
     for i in (0, 1):
         z_copies[i].wait_recv()
         z_copies[i + 2].start()
         along(i + 1)
     turn(0)
-    attend(3, 0)
-    attend(1, 0)
-    attend(0, 3)
+    attend((3, 0), (1, 0))
     z_copies[2].wait_recv()
     z_copies[3].wait_recv()
     along(3)
-    attend(0, 1)
+    attend((0, 3), (0, 1))
     turn(1)
     gather.until(1000.0)
-    attend(3, 3)
     turn(2)
-    attend(3, 1)
-    attend(2, 0)
-    attend(1, 3)
+    attend((3, 3), (3, 1))
+    attend((2, 0))
     turn(3)
-    attend(1, 1)
-    attend(2, 3)
-    attend(2, 1)
+    attend((1, 3), (1, 1))
+    attend((2, 3), (2, 1))
     for j in range(4):
         for i in (2, 3):
             sets[j][i].wait_recv()
-        attend(turns[j], 2)
+        if j % 2:
+            attend((turns[j - 1], 2), (turns[j], 2))
     for head in range(4):
         rows = pl.ds(256 * head, 256)
         attn[:, pl.ds(128 * head, 128)] = (mix[rows] / tot[rows]).astype(BF)
@@ -804,7 +807,7 @@
     trail_copies = [remote(trail, trail_in.at[t], trail_send, trail_recv.at[t], next_first) for t in range(4)]
     for t in range(4):
 
-        @pl.when(tp == t)
+        @pl.when((tp == t) & (ctx < 15))
         def _():
             trail_copies[t].start()
 
@@ -814,7 +817,7 @@
     result = hidden[...].astype(F32) + dot((c256 == slot_col).astype(BF), patch_out)
     out[...] = result.astype(BF)
 
-    @pl.when(tp == 0)
+    @pl.when((tp == 0) & (ctx > 0))
     def _():
         row = jnp.zeros((1, 1024), F32)
         for t in range(4):
@@ -822,7 +825,9 @@
             row = row + trail_in[t][0:1].astype(F32)
         out[...] = (out[...].astype(F32) + jnp.where(run_col == 0.0, row, F32(0.0))).astype(BF)
 
-    trail_copies[0].wait_send()
+    @pl.when(ctx < 15)
+    def _():
+        trail_copies[0].wait_send()
 
     @pl.when(tp == 0)
     def _():

time: 220 us -> 211 us (0.959)
  the two profiles are of different devices: /device:TPU:32 before, /device:TPU:234 now
where the time goes in v2:
time: 211 us
  Pallas kernels  205 us (97%)
  local copies, waits for them, and re-layouts  4.43 us (2%)
    pallas_call x1, Pallas kernels, second_stage(): pl.pallas_call(second_kernel, out_shape=jax.ShapeDtypeStruct(hidden.shape...  149 us
    pallas_call x1, Pallas kernels, first_stage(): pl.pallas_call(first_kernel, out_shape=(jax.ShapeDtypeStruct((4, 4, FIRST...  56.1 us

profile of v2, /device:TPU:234, one launch (start us, length us, event | category | flops | bytes accessed | tf_op | source)
XLA Modules:
  0.0 210.6 jit_solution(16030410429667498524)
XLA Ops:
  0.0 1.4 fusion
  1.4 1.2 broadcast_in_dim.10.count
  2.6 0.6 broadcast_in_dim.23.marks_row
  3.2 0.7 broadcast_in_dim.24.marks_col
  4.0 56.1 %shard_map.118 = (bf16[4,4,1024,256]{3,2,1,0:T(8,128)(2,1)}, bf16[256,1024]{1,0:T(8,128)(2,1)}, s32[4,8,128]{2,1,0:T(8,128)}) custom-call(bf16[64,1024]{1,0:T(8,128)(2,1)} %up.1, bf16[256,512]{1,0:T(8,128)(2,1)} %query_w.1, bf16[256,128]{1,0:T(8,128)(2,1)} %key_w.1, bf16[256,128]{1,0:T(8,128)(2,1)} %value_w.1, bf16[256,1024]{1,0:T(8,128)(2,1)} %embed.1, ...), custom_call_target="tpu_custom_call" | custom-call | tf_op jit(solution)/shard_map/pallas_call | solution.py:420
  60.0 148.7 %shard_map.119 = bf16[256,1024]{1,0:T(8,128)(2,1)} custom-call(bf16[256,1024]{1,0:T(8,128)(2,1)} %get-tuple-element.8.hidden, bf16[16,256]{1,0:T(8,128)(2,1)} %broadcast_in_dim.23.marks_row, bf16[256,128]{1,0:T(8,128)(2,1)} %broadcast_in_dim.24.marks_col, s32[4,8,128]{2,1,0:T(8,128)} %get-tuple-element.9.counts, f32[1,4096]{1,0:T(1,128)} %bitcast.4, ...), custom_call_target="tpu_custom_call" | custom-call | tf_op jit(solution)/shard_map/pallas_call | solution.py:859
  208.7 1.9 copy.14
